TPU v7x, 32 devices: a whole 2x2x4 slice. The times are simulated.
32 devices in a mesh: mod: 4 (over y, x), seq: 8 (over z, core).
Axes of the slice: x: 2, y: 2, z: 4, core: 2. Of those that a mesh axis runs over, the one named last changes fastest.
Arguments:
- tokens: bfloat16 [2048, 4096], P(('mod', 'seq')), may hold values from -6 to 6
- norm_gain: float32 [3, 4096], replicated, may hold values from 0.2 to 2.6
- qkv_weight: bfloat16 [3, 4096, 12288], P(None, None, 'seq'), may hold values from -0.45 to 0.45
- out_weight: bfloat16 [3, 4096, 4096], P(None, 'seq'), may hold values from -0.375 to 0.375
- modality: int32 [16], replicated, may hold values from 0 to 2
- doc_lengths: int32 [4], replicated, may hold values from 1 to 1024, 2048 in all
Outputs:
- mixed: bfloat16 [2048, 4096], P(('mod', 'seq'))
Inputs may be any that keep to these rules, and one draw needn't show every extreme that they name: `doc_lengths`: the lengths sum to 2048; documents follow one another from position 0 in the given order.
All inputs are finite; a program needn't handle non-finite values.
Results may differ from a plain program's by a relative error of at most 0.015.
Values may be sent and summed in bfloat16 or wider, within the bound.
A program may use at most 128 MiB of HBM per device.

v0:
```python
import math
import jax
import jax.numpy as jnp
from jax import lax
from jax.sharding import PartitionSpec as P

HDIM = 128
BLOCK = 128


def modes_of_rows(first_row, row_count, modality):
    block_ids = (first_row + jnp.arange(row_count, dtype=jnp.int32)) // BLOCK
    block_table = jnp.arange(modality.shape[0], dtype=jnp.int32)
    picked = jnp.where(block_ids[:, None] == block_table[None, :], modality[None, :], 0)
    return jnp.sum(picked, axis=1)


def documents(positions, doc_lengths):
    doc_ends = jnp.cumsum(doc_lengths)
    return jnp.sum((positions[:, None] >= doc_ends[None, :]).astype(jnp.int32), axis=1)


def body(tokens, norm_gain, qkv_weight, out_weight, modality, doc_lengths):
    row_count = tokens.shape[0]
    seq_count = lax.axis_size("seq")
    mod_count = lax.axis_size("mod")
    group_rows = row_count * seq_count
    mod_index = lax.axis_index("mod")
    own_first = (mod_index * seq_count + lax.axis_index("seq")) * row_count
    row_modes = modes_of_rows(own_first, row_count, modality)
    choose = (
        row_modes[:, None, None] == jnp.arange(norm_gain.shape[0], dtype=jnp.int32)[None, :, None]
    )
    gain_rows = jnp.sum(jnp.where(choose, norm_gain[None, :, :], 0.0), axis=1)
    values = tokens.astype(jnp.float32)
    mean_square = jnp.mean(values * values, axis=1, keepdims=True)
    normed = (values * lax.rsqrt(mean_square + 1e-05) * gain_rows).astype(jnp.bfloat16)
    gathered = lax.all_gather(normed, "seq", axis=0, tiled=True)
    group_first = mod_index * group_rows
    block_count = group_rows // BLOCK
    block_modes = lax.dynamic_slice_in_dim(modality, group_first // BLOCK, block_count)
    heads_here = qkv_weight.shape[2] // (3 * HDIM)

    def project(block_pair):
        row_block, block_mode = block_pair
        weight = lax.dynamic_index_in_dim(qkv_weight, block_mode, 0, keepdims=False)
        return jnp.dot(row_block, weight, preferred_element_type=jnp.float32).astype(jnp.bfloat16)

    projected = lax.map(
        project, (gathered.reshape(block_count, BLOCK, gathered.shape[1]), block_modes)
    )
    projected = projected.reshape(group_rows, heads_here, 3, HDIM)
    queries = projected[:, :, 0, :]
    keys_here = projected[:, :, 1, :]
    values_here = projected[:, :, 2, :]
    quarter = group_rows // mod_count
    local_rows = jnp.arange(group_rows, dtype=jnp.int32)
    query_pos = group_first + local_rows
    query_docs = documents(query_pos, doc_lengths)
    block_size = min(512, quarter)
    block_total = group_rows // block_size
    score_scale = 1.0 / math.sqrt(HDIM)
    query_blocks = queries.reshape(block_total, block_size, heads_here, HDIM)
    pos_blocks = query_pos.reshape(block_total, block_size)
    doc_blocks = query_docs.reshape(block_total, block_size)
    start_state = (
        jnp.full((block_total, heads_here, block_size), -1e30, jnp.float32),
        jnp.zeros((block_total, heads_here, block_size), jnp.float32),
        jnp.zeros((block_total, block_size, heads_here, HDIM), jnp.float32),
    )
    key_start = jnp.int32(0)
    piece_keys = lax.all_gather(keys_here, "mod", axis=0, tiled=True)
    piece_values = lax.all_gather(values_here, "mod", axis=0, tiled=True)
    key_count = piece_keys.shape[0]
    key_pos = jnp.arange(key_count, dtype=jnp.int32)
    key_docs = documents(key_pos, doc_lengths)

    def one_block(block_state):
        row_max, totals, summed_rows, query_block, block_pos, block_docs = block_state

        def attend(unused):
            scores = (
                jnp.einsum(
                    "qhc,khc->hqk", query_block, piece_keys, preferred_element_type=jnp.float32
                )
                * score_scale
            )
            allowed = (
                (key_pos[None, :] <= block_pos[:, None])
                & (key_docs[None, :] == block_docs[:, None])
            )[None, :, :]
            new_max = jnp.maximum(row_max, jnp.max(jnp.where(allowed, scores, -1e30), axis=2))
            weights = jnp.where(allowed, jnp.exp(scores - new_max[:, :, None]), 0.0)
            rescale = jnp.exp(row_max - new_max)
            new_totals = totals * rescale + jnp.sum(weights, axis=2)
            added_rows = jnp.einsum(
                "hqk,khc->qhc",
                weights.astype(jnp.bfloat16),
                piece_values,
                preferred_element_type=jnp.float32,
            )
            new_rows = summed_rows * jnp.transpose(rescale)[:, :, None] + added_rows
            return (new_max, new_totals, new_rows)

        def keep_state(unused):
            return (row_max, totals, summed_rows)

        return lax.cond(key_start <= jnp.max(block_pos), attend, keep_state, 0)

    row_max, totals, summed_rows = lax.map(
        one_block,
        (start_state[0], start_state[1], start_state[2], query_blocks, pos_blocks, doc_blocks),
    )
    divisor = jnp.transpose(totals, (0, 2, 1))[:, :, :, None]
    attended = (summed_rows / divisor).astype(jnp.bfloat16).reshape(group_rows, heads_here * HDIM)

    def output(block_pair):
        row_block, block_mode = block_pair
        weight = lax.dynamic_index_in_dim(out_weight, block_mode, 0, keepdims=False)
        return jnp.dot(row_block, weight, preferred_element_type=jnp.float32)

    partial_value = lax.map(
        output, (attended.reshape(block_count, BLOCK, attended.shape[1]), block_modes)
    )
    head_sums = lax.psum_scatter(
        partial_value.reshape(group_rows, partial_value.shape[2]).astype(jnp.bfloat16),
        "seq",
        scatter_dimension=0,
        tiled=True,
    ).astype(jnp.float32)
    return (tokens.astype(jnp.float32) + head_sums).astype(jnp.bfloat16)


def solution(mesh):
    return jax.shard_map(
        body,
        mesh=mesh,
        in_specs=(
            P(("mod", "seq"), None),
            P(),
            P(None, None, "seq"),
            P(None, "seq", None),
            P(),
            P(),
        ),
        out_specs=P(("mod", "seq"), None),
        check_vma=False,
    )
```

profile of v0, /device:TPU:0, one launch (start us, length us, event | category | flops | bytes accessed | tf_op | source)
XLA Modules:
  0.0 286.2 jit_solution(8059738032792153300)
XLA Ops:
  7.4 1.2 fusion.48
  8.6 1.3 select_reduce_fusion.1
  9.9 2.0 fusion.50
  12.2 49.6 %all-gather.6.cloned.1.call-done = bf16[512,4096]{1,0:T(8,128)(2,1)} async-done(((bf16[64,4096]{1,0:T(8,128)(2,1)}), bf16[512,4096]{1,0:T(8,128)(2,1)}) %all-gather.6.cloned.1.call-update) | async-done | bytes 4194320 | tf_op jit(solution)/shard_map/all_gather | solution.py:38
  61.7 37.1 %while.33 = (s32[]{:T(128)}, bf16[4,128,1536]{2,1,0:T(8,128)(2,1)S(1)}, bf16[4,128,4096]{2,1,0:T(8,128)(2,1)}, s32[4]{0:T(128)S(1)}, bf16[3,4096,1536]{2,1,0:T(8,128)(2,1)}, /*index=5*/s32[]{:T(128)}, s32[]{:T(128)}, s32[]{:T(128)}) while((s32[]{:T(128)}, bf16[4,128,1536]{2,1,0:T(8,128)(2,1)S(1)}, bf16[4,128,4096]{2,1,0:T(8,128)(2,1)}, ...), condition=%wide.region_4.5_spmd, body=%wide.region_3.4_spmd.sunk | while | flops 1610809344 | bytes 14025863 | solution.py:49
  64.3 6.7 %fusion.65 = bf16[4,128,1536]{2,1,0:T(8,128)(2,1)S(1)} fusion(bf16[4,128,1536]{2,1,0:T(8,128)(2,1)S(1)} %get-tuple-element.457, s32[]{:T(128)} %get-tuple-element.456, bf16[3,4096,1536]{2,1,0:T(8,128)(2,1)} %get-tuple-element.468, s32[]{:T(128)S(6)} %select_n.67, bf16[4,128,4096]{2,1,0:T(8,128)(2,1)} %get-tuple-element.466), kind=kOutput, calls=%fused_computation.6.clone.1 | convolution fusion | flops 1610809344 | bytes 14025732 | tf_op jit(solution)/shard_map/while/body/eval_jaxpr/dot_general | solution.py:47
  73.5 6.7 %fusion.65 = bf16[4,128,1536]{2,1,0:T(8,128)(2,1)S(1)} fusion(bf16[4,128,1536]{2,1,0:T(8,128)(2,1)S(1)} %get-tuple-element.457, s32[]{:T(128)} %get-tuple-element.456, bf16[3,4096,1536]{2,1,0:T(8,128)(2,1)} %get-tuple-element.468, s32[]{:T(128)S(6)} %select_n.67, bf16[4,128,4096]{2,1,0:T(8,128)(2,1)} %get-tuple-element.466), kind=kOutput, calls=%fused_computation.6.clone.1 | convolution fusion | flops 1610809344 | bytes 14025732 | tf_op jit(solution)/shard_map/while/body/eval_jaxpr/dot_general | solution.py:47
  82.8 6.7 %fusion.65 = bf16[4,128,1536]{2,1,0:T(8,128)(2,1)S(1)} fusion(bf16[4,128,1536]{2,1,0:T(8,128)(2,1)S(1)} %get-tuple-element.457, s32[]{:T(128)} %get-tuple-element.456, bf16[3,4096,1536]{2,1,0:T(8,128)(2,1)} %get-tuple-element.468, s32[]{:T(128)S(6)} %select_n.67, bf16[4,128,4096]{2,1,0:T(8,128)(2,1)} %get-tuple-element.466), kind=kOutput, calls=%fused_computation.6.clone.1 | convolution fusion | flops 1610809344 | bytes 14025732 | tf_op jit(solution)/shard_map/while/body/eval_jaxpr/dot_general | solution.py:47
  92.1 6.7 %fusion.65 = bf16[4,128,1536]{2,1,0:T(8,128)(2,1)S(1)} fusion(bf16[4,128,1536]{2,1,0:T(8,128)(2,1)S(1)} %get-tuple-element.457, s32[]{:T(128)} %get-tuple-element.456, bf16[3,4096,1536]{2,1,0:T(8,128)(2,1)} %get-tuple-element.468, s32[]{:T(128)S(6)} %select_n.67, bf16[4,128,4096]{2,1,0:T(8,128)(2,1)} %get-tuple-element.466), kind=kOutput, calls=%fused_computation.6.clone.1 | convolution fusion | flops 1610809344 | bytes 14025732 | tf_op jit(solution)/shard_map/while/body/eval_jaxpr/dot_general | solution.py:47
  103.3 32.5 %all-gather.8.cloned.1.call-done = bf16[2048,4,1,128]{0,3,2,1:T(8,128)(2,1)} async-done(((bf16[512,4,1,128]{0,3,2,1:T(8,128)(2,1)}), bf16[2048,4,1,128]{0,3,2,1:T(8,128)(2,1)}) %all-gather.8.cloned.1.call-update) | async-done | bytes 2097168 | tf_op jit(solution)/shard_map/all_gather | solution.py:72
  135.7 3.0 %copy.17 = bf16[2048,4,128]{2,0,1:T(8,128)(2,1)S(1)} copy(bf16[2048,4,128]{0,2,1:T(8,128)(2,1)} %bitcast.85) | data formatting | bytes 4194304
  138.8 33.9 %all-gather.10.cloned.1.call-done = bf16[2048,4,1,128]{0,3,2,1:T(8,128)(2,1)} async-done(((bf16[512,4,1,128]{0,3,2,1:T(8,128)(2,1)}), bf16[2048,4,1,128]{0,3,2,1:T(8,128)(2,1)}) %all-gather.10.cloned.1.call-update) | async-done | bytes 2097168 | tf_op jit(solution)/shard_map/all_gather | solution.py:73
  172.7 4.0 %copy.18 = bf16[2048,4,128]{2,0,1:T(8,128)(2,1)} copy(bf16[2048,4,128]{0,2,1:T(8,128)(2,1)} %bitcast.86) | data formatting | bytes 4194304
  176.6 23.8 %while.35 = (s32[]{:T(128)}, f32[4,4,128]{2,1,0:T(4,128)S(1)}, f32[4,128,4,128]{1,3,2,0:T(8,128)}, s32[4,128]{1,0:T(4,128)S(1)}, s32[2048]{0:T(1024)S(1)}, /*ind...) while((s32[]{:T(128)}, f32[4,4,128]{2,1,0:T(4,128)S(1)}, ...), condition=%wide.region_14.15_spmd.clone, body=%wide.region_8.14_spmd.clone.sunk | while | flops 549324416 | bytes 28503860 | solution.py:110
  178.0 3.7 %conditional.3 = (f32[1,4,128]{2,1,0:T(4,128)S(1)}, f32[1,128,4,128]{3,1,2,0:T(8,128)S(1)}) conditional(s32[]{:T(128)} %convert_element_type.82, (f32[4,128]{1,0:T(4,128)S(1)}, f32[128,4,128]{2,0,1:T(8,128)S(1)}) %tuple.105, (s32[2048]{0:T(1024)S(1)}, s32[1,128]{1,0:T(1,128)S(1)}, s32[2048]{0:T(1024)S(1)}, s32[4,128]{1,0:T(4,128)S(1)}, s32[]{:T(128)}, ...), branch_computations={%region_10.10_spmd, %region_11.13_spmd} | conditional | flops 549324288 | bytes 26912820 | solution.py:108
  179.3 1.2 fusion.18
  180.5 1.2 fusion.31
  183.9 3.7 %conditional.3 = (f32[1,4,128]{2,1,0:T(4,128)S(1)}, f32[1,128,4,128]{3,1,2,0:T(8,128)S(1)}) conditional(s32[]{:T(128)} %convert_element_type.82, (f32[4,128]{1,0:T(4,128)S(1)}, f32[128,4,128]{2,0,1:T(8,128)S(1)}) %tuple.105, (s32[2048]{0:T(1024)S(1)}, s32[1,128]{1,0:T(1,128)S(1)}, s32[2048]{0:T(1024)S(1)}, s32[4,128]{1,0:T(4,128)S(1)}, s32[]{:T(128)}, ...), branch_computations={%region_10.10_spmd, %region_11.13_spmd} | conditional | flops 549324288 | bytes 26912820 | solution.py:108
  185.2 1.2 fusion.18
  186.4 1.2 fusion.31
  189.8 3.7 %conditional.3 = (f32[1,4,128]{2,1,0:T(4,128)S(1)}, f32[1,128,4,128]{3,1,2,0:T(8,128)S(1)}) conditional(s32[]{:T(128)} %convert_element_type.82, (f32[4,128]{1,0:T(4,128)S(1)}, f32[128,4,128]{2,0,1:T(8,128)S(1)}) %tuple.105, (s32[2048]{0:T(1024)S(1)}, s32[1,128]{1,0:T(1,128)S(1)}, s32[2048]{0:T(1024)S(1)}, s32[4,128]{1,0:T(4,128)S(1)}, s32[]{:T(128)}, ...), branch_computations={%region_10.10_spmd, %region_11.13_spmd} | conditional | flops 549324288 | bytes 26912820 | solution.py:108
  192.3 1.2 fusion.31
  195.8 3.7 %conditional.3 = (f32[1,4,128]{2,1,0:T(4,128)S(1)}, f32[1,128,4,128]{3,1,2,0:T(8,128)S(1)}) conditional(s32[]{:T(128)} %convert_element_type.82, (f32[4,128]{1,0:T(4,128)S(1)}, f32[128,4,128]{2,0,1:T(8,128)S(1)}) %tuple.105, (s32[2048]{0:T(1024)S(1)}, s32[1,128]{1,0:T(1,128)S(1)}, s32[2048]{0:T(1024)S(1)}, s32[4,128]{1,0:T(4,128)S(1)}, s32[]{:T(128)}, ...), branch_computations={%region_10.10_spmd, %region_11.13_spmd} | conditional | flops 549324288 | bytes 26912820 | solution.py:108
  198.3 1.2 fusion.31
  200.4 1.3 divide_convert_fusion
  201.7 25.9 %while.34 = (s32[]{:T(128)}, bf16[4,128,4096]{2,1,0:T(8,128)(2,1)}, bf16[4,128,512]{1,2,0:T(8,128)(2,1)S(1)}, s32[4]{0:T(128)S(1)}, bf16[3,512,4096]{2,1,0:T(8,128)(2,1)}, /*index=5*/s32[]{:T(128)}, s32[]{:T(128)}, s32[]{:T(128)}) while((s32[]{:T(128)}, bf16[4,128,4096]{2,1,0:T(8,128)(2,1)}, bf16[4,128,512]{1,2,0:T(8,128)(2,1)S(1)}, ...), condition=%wide.region_16.17_spmd, body=%wide.region_15.16_spmd.sunk | while | flops 536870912 | bytes 6423687 | solution.py:122
  204.3 3.9 %fusion.68 = bf16[4,128,4096]{2,1,0:T(8,128)(2,1)} fusion(bf16[4,128,4096]{2,1,0:T(8,128)(2,1)} %get-tuple-element.517, s32[]{:T(128)} %get-tuple-element.516, bf16[3,512,4096]{2,1,0:T(8,128)(2,1)} %get-tuple-element.528, s32[]{:T(128)S(6)} %select_n.68, bf16[4,128,512]{1,2,0:T(8,128)(2,1)S(1)} %get-tuple-element.526), kind=kOutput, calls=%fused_computation.36.clone.1 | convolution fusion | flops 536870912 | bytes 6423556 | tf_op jit(solution)/shard_map/while/body/eval_jaxpr/dot_general | solution.py:120
  210.7 4.0 %fusion.68 = bf16[4,128,4096]{2,1,0:T(8,128)(2,1)} fusion(bf16[4,128,4096]{2,1,0:T(8,128)(2,1)} %get-tuple-element.517, s32[]{:T(128)} %get-tuple-element.516, bf16[3,512,4096]{2,1,0:T(8,128)(2,1)} %get-tuple-element.528, s32[]{:T(128)S(6)} %select_n.68, bf16[4,128,512]{1,2,0:T(8,128)(2,1)S(1)} %get-tuple-element.526), kind=kOutput, calls=%fused_computation.36.clone.1 | convolution fusion | flops 536870912 | bytes 6423556 | tf_op jit(solution)/shard_map/while/body/eval_jaxpr/dot_general | solution.py:120
  217.3 3.9 %fusion.68 = bf16[4,128,4096]{2,1,0:T(8,128)(2,1)} fusion(bf16[4,128,4096]{2,1,0:T(8,128)(2,1)} %get-tuple-element.517, s32[]{:T(128)} %get-tuple-element.516, bf16[3,512,4096]{2,1,0:T(8,128)(2,1)} %get-tuple-element.528, s32[]{:T(128)S(6)} %select_n.68, bf16[4,128,512]{1,2,0:T(8,128)(2,1)S(1)} %get-tuple-element.526), kind=kOutput, calls=%fused_computation.36.clone.1 | convolution fusion | flops 536870912 | bytes 6423556 | tf_op jit(solution)/shard_map/while/body/eval_jaxpr/dot_general | solution.py:120
  223.7 3.9 %fusion.68 = bf16[4,128,4096]{2,1,0:T(8,128)(2,1)} fusion(bf16[4,128,4096]{2,1,0:T(8,128)(2,1)} %get-tuple-element.517, s32[]{:T(128)} %get-tuple-element.516, bf16[3,512,4096]{2,1,0:T(8,128)(2,1)} %get-tuple-element.528, s32[]{:T(128)S(6)} %select_n.68, bf16[4,128,512]{1,2,0:T(8,128)(2,1)S(1)} %get-tuple-element.526), kind=kOutput, calls=%fused_computation.36.clone.1 | convolution fusion | flops 536870912 | bytes 6423556 | tf_op jit(solution)/shard_map/while/body/eval_jaxpr/dot_general | solution.py:120
  227.7 50.1 %reduce-scatter.2.cloned.1.call-done = bf16[64,4096]{1,0:T(8,128)(2,1)} async-done(((bf16[512,4096]{1,0:T(8,128)(2,1)}), bf16[64,4096]{1,0:T(8,128)(2,1)}) %reduce-scatter.2.cloned.1.call-update) | async-done | bytes 524304 | tf_op jit(solution)/shard_map/reduce_scatter | solution.py:125
  277.8 2.0 fusion.51
  (107 shorter events, 23.7 us)
Async XLA Ops:
  6.5 5.5 %copy-start.2 = (s32[16]{0:T(128)S(1)}, s32[16]{0:T(128)}, u32[]{:S(2)}) copy-start(s32[16]{0:T(128)} %param.18) | copy-start | bytes 196
  6.5 55.2 %all-gather.6.cloned.1.call-start = ((), (), s32[]{:S(2)}) async-start(), calls=%async_computation.1 | async-start | bytes 4718592 | tf_op jit(solution)/shard_map/all_gather | solution.py:38
  12.0 123.8 %all-gather.8.cloned.1.call-start = ((), (), s32[]{:S(2)}) async-start(), calls=%async_computation.3 | async-start | bytes 2621440 | tf_op jit(solution)/shard_map/all_gather | solution.py:72
  99.9 2.6 copy-start.3
  101.7 70.9 %all-gather.10.cloned.1.call-start = ((), (), s32[]{:S(2)}) async-start(), calls=%async_computation.4 | async-start | bytes 2621440 | tf_op jit(solution)/shard_map/all_gather | solution.py:73
  102.5 175.3 %reduce-scatter.2.cloned.1.call-start = ((), (), s32[]{:S(2)}) async-start(), calls=%async_computation.2 | async-start | bytes 4718592 | tf_op jit(solution)/shard_map/reduce_scatter | solution.py:125
  178.3 2.2 copy-start.1
  184.2 2.2 copy-start.1
  190.2 2.2 copy-start.1
  196.1 2.2 copy-start.1
  227.6 50.1 %copy-start = (bf16[64,4096]{1,0:T(8,128)(2,1)S(1)}, bf16[64,4096]{1,0:T(8,128)(2,1)}, u32[]{:S(2)}) copy-start(bf16[64,4096]{1,0:T(8,128)(2,1)} %param.14) | copy-start | bytes 1572868
Sparse Core Ops, SparseCore 0:
  12.1 49.5 all-gather.5
  101.9 33.8 all-gather.7
  137.6 35.0 all-gather.9
  227.8 49.9 reduce-scatter.1
where the time goes:
time: 287 us; the launch traced here: 286 us
  waiting for transfers between devices  167 us (58%)
  matrix products  51.3 us (18%)
  local copies, waits for them, and re-layouts  18.7 us (7%)
  loops' own time  18.6 us (6%)
  other arithmetic  17.4 us (6%)
  between operations  13.3 us (5%)
    reduce_scatter x1, waiting for transfers between devices, body(): lax.psum_scatter(partial_value.reshape(group_rows, partial_value.shape[2]...  50.1 us
    all_gather x1, waiting for transfers between devices, body(): gathered = lax.all_gather(normed, 'seq', axis=0, tiled=True)  49.6 us
    all_gather x1, waiting for transfers between devices, body(): piece_values = lax.all_gather(values_here, 'mod', axis=0, tiled=True)  33.9 us
    all_gather x1, waiting for transfers between devices, body(): piece_keys = lax.all_gather(keys_here, 'mod', axis=0, tiled=True)  32.5 us
    dot_general x4, matrix products, project(): jnp.dot(row_block, weight, preferred_element_type=jnp.float32)  26.9 us
    dot_general x4, matrix products, output(): return jnp.dot(row_block, weight, preferred_element_type=jnp.float32)  15.8 us
    another operation x1, loops' own time, body(): lax.map(project, (gathered.reshape(block_count, BLOCK, gathered.shape[1])...  7.85 us
    another operation x1, loops' own time, body(): lax.map(output, (attended.reshape(block_count, BLOCK, attended.shape[1]),...  7.79 us
  transfers between devices with their start and end apart: 4, of which 4 were waited for; matrix products, arithmetic and copies ran while one was open for 1% of the time, Pallas kernels for 0%

commit v1 on v0

--- a/solution.py
+++ b/solution.py
@@ -69,7 +69,12 @@
         jnp.zeros((block_total, block_size, heads_here, HDIM), jnp.float32),
     )
     key_start = jnp.int32(0)
-    piece_keys = lax.all_gather(keys_here, "mod", axis=0, tiled=True)
+    ring = [keys_here]
+    for hop in range(3):
+        ring.append(lax.ppermute(ring[-1], "mod", [(dev, (dev + 1) % 4) for dev in range(4)]))
+    piece_keys = jnp.roll(
+        jnp.concatenate(ring[::-1], axis=0), (lax.axis_index("mod") + 1) * ring[0].shape[0], axis=0
+    )
     piece_values = lax.all_gather(values_here, "mod", axis=0, tiled=True)
     key_count = piece_keys.shape[0]
     key_pos = jnp.arange(key_count, dtype=jnp.int32)

time: 287 us -> 278 us (0.969)
  waiting for transfers between devices: 167 us -> 148 us
  local copies, waits for them, and re-layouts: 18.7 us -> 24.5 us
  starting transfers between devices: 0.12 us -> 3.43 us
    ppermute x0 -> x3, waiting for transfers between devices: none -> 50.1 us  [body(): lax.ppermute(ring[-1], 'mod', [(dev, (dev + 1) % 4) for dev in range(4)])]
    all_gather x1, waiting for transfers between devices: 33.9 us -> 0.02 us  [body(): piece_values = lax.all_gather(values_here, 'mod', axis=0, tiled=True)]
    all_gather x1 -> x0, waiting for transfers between devices: 32.5 us -> none  [body(): piece_keys = lax.all_gather(keys_here, 'mod', axis=0, tiled=True)]
    unnamed x9 -> x16, local copies, waits for them, and re-layouts: 7.05 us -> 10.6 us
    ppermute x0 -> x3, starting transfers between devices: none -> 3.34 us  [body(): lax.ppermute(ring[-1], 'mod', [(dev, (dev + 1) % 4) for dev in range(4)])]
  transfers between devices with their start and end apart: 4 -> 6, of which waited for: 4 -> 5; matrix products, arithmetic and copies ran while one was open for 1% -> 4% of each run, Pallas kernels for 0% -> 0%
where the time goes in v1:
time: 278 us; the launch traced here: 276 us
  waiting for transfers between devices  148 us (53%)
  matrix products  51.3 us (18%)
  local copies, waits for them, and re-layouts  24.5 us (9%)
  loops' own time  18.6 us (7%)
  other arithmetic  17.4 us (6%)
  between operations  13.3 us (5%)
  starting transfers between devices  3.43 us (1%)
    ppermute x3, waiting for transfers between devices, body(): lax.ppermute(ring[-1], 'mod', [(dev, (dev + 1) % 4) for dev in range(4)])  50.1 us
    all_gather x1, waiting for transfers between devices, body(): gathered = lax.all_gather(normed, 'seq', axis=0, tiled=True)  49.6 us
    reduce_scatter x1, waiting for transfers between devices, body(): lax.psum_scatter(partial_value.reshape(group_rows, partial_value.shape[2]...  48.1 us
    dot_general x4, matrix products, project(): jnp.dot(row_block, weight, preferred_element_type=jnp.float32)  26.9 us
    dot_general x4, matrix products, output(): return jnp.dot(row_block, weight, preferred_element_type=jnp.float32)  15.8 us
    unnamed x16, local copies, waits for them, and re-layouts  10.6 us
    another operation x1, loops' own time, body(): lax.map(project, (gathered.reshape(block_count, BLOCK, gathered.shape[1])...  7.85 us
    another operation x1, loops' own time, body(): lax.map(output, (attended.reshape(block_count, BLOCK, attended.shape[1]),...  7.79 us
  transfers between devices with their start and end apart: 6, of which 5 were waited for; matrix products, arithmetic and copies ran while one was open for 4% of the time, Pallas kernels for 0%

profile of v1, /device:TPU:0, one launch (start us, length us, event | category | flops | bytes accessed | tf_op | source)
XLA Modules:
  0.0 276.5 jit_solution(1304843077935975693)
XLA Ops:
  7.4 1.2 fusion.48
  8.6 1.3 select_reduce_fusion.1
  9.9 2.0 fusion.50
  12.2 49.6 %all-gather.4.cloned.1.call-done = bf16[512,4096]{1,0:T(8,128)(2,1)} async-done(((bf16[64,4096]{1,0:T(8,128)(2,1)}), bf16[512,4096]{1,0:T(8,128)(2,1)}) %all-gather.4.cloned.1.call-update) | async-done | bytes 4194320 | tf_op jit(solution)/shard_map/all_gather | solution.py:38
  61.7 37.1 %while.33 = (s32[]{:T(128)}, bf16[4,128,1536]{2,1,0:T(8,128)(2,1)S(1)}, bf16[4,128,4096]{2,1,0:T(8,128)(2,1)}, s32[4]{0:T(128)S(1)}, bf16[3,4096,1536]{2,1,0:T(8,128)(2,1)}, /*index=5*/s32[]{:T(128)}, s32[]{:T(128)}, s32[]{:T(128)}) while((s32[]{:T(128)}, bf16[4,128,1536]{2,1,0:T(8,128)(2,1)S(1)}, bf16[4,128,4096]{2,1,0:T(8,128)(2,1)}, ...), condition=%wide.region_4.5_spmd, body=%wide.region_3.4_spmd.sunk | while | flops 1610809344 | bytes 14025863 | solution.py:49
  64.3 6.7 %fusion.65 = bf16[4,128,1536]{2,1,0:T(8,128)(2,1)S(1)} fusion(bf16[4,128,1536]{2,1,0:T(8,128)(2,1)S(1)} %get-tuple-element.457, s32[]{:T(128)} %get-tuple-element.456, bf16[3,4096,1536]{2,1,0:T(8,128)(2,1)} %get-tuple-element.468, s32[]{:T(128)S(6)} %select_n.81, bf16[4,128,4096]{2,1,0:T(8,128)(2,1)} %get-tuple-element.466), kind=kOutput, calls=%fused_computation.6.clone.1 | convolution fusion | flops 1610809344 | bytes 14025732 | tf_op jit(solution)/shard_map/while/body/eval_jaxpr/dot_general | solution.py:47
  73.5 6.7 %fusion.65 = bf16[4,128,1536]{2,1,0:T(8,128)(2,1)S(1)} fusion(bf16[4,128,1536]{2,1,0:T(8,128)(2,1)S(1)} %get-tuple-element.457, s32[]{:T(128)} %get-tuple-element.456, bf16[3,4096,1536]{2,1,0:T(8,128)(2,1)} %get-tuple-element.468, s32[]{:T(128)S(6)} %select_n.81, bf16[4,128,4096]{2,1,0:T(8,128)(2,1)} %get-tuple-element.466), kind=kOutput, calls=%fused_computation.6.clone.1 | convolution fusion | flops 1610809344 | bytes 14025732 | tf_op jit(solution)/shard_map/while/body/eval_jaxpr/dot_general | solution.py:47
  82.8 6.7 %fusion.65 = bf16[4,128,1536]{2,1,0:T(8,128)(2,1)S(1)} fusion(bf16[4,128,1536]{2,1,0:T(8,128)(2,1)S(1)} %get-tuple-element.457, s32[]{:T(128)} %get-tuple-element.456, bf16[3,4096,1536]{2,1,0:T(8,128)(2,1)} %get-tuple-element.468, s32[]{:T(128)S(6)} %select_n.81, bf16[4,128,4096]{2,1,0:T(8,128)(2,1)} %get-tuple-element.466), kind=kOutput, calls=%fused_computation.6.clone.1 | convolution fusion | flops 1610809344 | bytes 14025732 | tf_op jit(solution)/shard_map/while/body/eval_jaxpr/dot_general | solution.py:47
  92.1 6.7 %fusion.65 = bf16[4,128,1536]{2,1,0:T(8,128)(2,1)S(1)} fusion(bf16[4,128,1536]{2,1,0:T(8,128)(2,1)S(1)} %get-tuple-element.457, s32[]{:T(128)} %get-tuple-element.456, bf16[3,4096,1536]{2,1,0:T(8,128)(2,1)} %get-tuple-element.468, s32[]{:T(128)S(6)} %select_n.81, bf16[4,128,4096]{2,1,0:T(8,128)(2,1)} %get-tuple-element.466), kind=kOutput, calls=%fused_computation.6.clone.1 | convolution fusion | flops 1610809344 | bytes 14025732 | tf_op jit(solution)/shard_map/while/body/eval_jaxpr/dot_general | solution.py:47
  101.6 1.5 collective-permute-start
  103.1 19.1 %collective-permute-done = bf16[512,4,128]{0,2,1:T(8,128)(2,1)S(1)} collective-permute-done((bf16[512,4,128]{0,2,1:T(8,128)(2,1)S(1)}, bf16[512,4,128]{0,2,1:T(8,128)(2,1)S(1)}, u32[]{:S(2)}, u32[]{:S(2)}) %collective-permute-start) | collective-permute-done | bytes 524320 | tf_op jit(solution)/shard_map/ppermute | solution.py:74
  122.8 22.3 %collective-permute-done.1 = bf16[512,4,128]{0,2,1:T(8,128)(2,1)S(1)} collective-permute-done((bf16[512,4,128]{0,2,1:T(8,128)(2,1)S(1)}, bf16[512,4,128]{0,2,1:T(8,128)(2,1)S(1)}, u32[]{:S(2)}, u32[]{:S(2)}) %collective-permute-start.1) | collective-permute-done | bytes 524320 | tf_op jit(solution)/shard_map/ppermute | solution.py:74
  145.0 1.3 collective-permute-start.2
  148.8 8.8 %collective-permute-done.2 = bf16[512,4,128]{0,2,1:T(8,128)(2,1)} collective-permute-done((bf16[512,4,128]{0,2,1:T(8,128)(2,1)S(1)}, bf16[512,4,128]{0,2,1:T(8,128)(2,1)}, u32[]{:S(2)}, u32[]{:S(2)}) %collective-permute-start.2) | collective-permute-done | bytes 524320 | tf_op jit(solution)/shard_map/ppermute | solution.py:74
  160.3 1.6 constant_dynamic-slice_fusion.2
  161.8 3.0 %copy.17 = bf16[2048,4,128]{2,0,1:T(8,128)(2,1)S(1)} copy(bf16[2048,4,128]{0,2,1:T(8,128)(2,1)} %constant_dynamic-slice_fusion.2) | data formatting | bytes 4194304
  164.9 4.0 %copy.18 = bf16[2048,4,128]{2,0,1:T(8,128)(2,1)} copy(bf16[2048,4,128]{0,2,1:T(8,128)(2,1)} %bitcast.90) | data formatting | bytes 4194304
  168.9 23.8 %while.35 = (s32[]{:T(128)}, f32[4,4,128]{2,1,0:T(4,128)S(1)}, f32[4,128,4,128]{1,3,2,0:T(8,128)}, s32[4,128]{1,0:T(4,128)S(1)}, s32[2048]{0:T(1024)S(1)}, /*ind...) while((s32[]{:T(128)}, f32[4,4,128]{2,1,0:T(4,128)S(1)}, ...), condition=%wide.region_14.15_spmd.clone, body=%wide.region_8.14_spmd.clone.sunk | while | flops 549324416 | bytes 28503860 | solution.py:115
  170.2 3.7 %conditional.3 = (f32[1,4,128]{2,1,0:T(4,128)S(1)}, f32[1,128,4,128]{3,1,2,0:T(8,128)S(1)}) conditional(s32[]{:T(128)} %convert_element_type.82, (f32[4,128]{1,0:T(4,128)S(1)}, f32[128,4,128]{2,0,1:T(8,128)S(1)}) %tuple.105, (s32[2048]{0:T(1024)S(1)}, s32[1,128]{1,0:T(1,128)S(1)}, s32[2048]{0:T(1024)S(1)}, s32[4,128]{1,0:T(4,128)S(1)}, s32[]{:T(128)}, ...), branch_computations={%region_10.10_spmd, %region_11.13_spmd} | conditional | flops 549324288 | bytes 26912820 | solution.py:113
  176.2 3.7 %conditional.3 = (f32[1,4,128]{2,1,0:T(4,128)S(1)}, f32[1,128,4,128]{3,1,2,0:T(8,128)S(1)}) conditional(s32[]{:T(128)} %convert_element_type.82, (f32[4,128]{1,0:T(4,128)S(1)}, f32[128,4,128]{2,0,1:T(8,128)S(1)}) %tuple.105, (s32[2048]{0:T(1024)S(1)}, s32[1,128]{1,0:T(1,128)S(1)}, s32[2048]{0:T(1024)S(1)}, s32[4,128]{1,0:T(4,128)S(1)}, s32[]{:T(128)}, ...), branch_computations={%region_10.10_spmd, %region_11.13_spmd} | conditional | flops 549324288 | bytes 26912820 | solution.py:113
  178.7 1.2 fusion.31
  182.1 3.7 %conditional.3 = (f32[1,4,128]{2,1,0:T(4,128)S(1)}, f32[1,128,4,128]{3,1,2,0:T(8,128)S(1)}) conditional(s32[]{:T(128)} %convert_element_type.82, (f32[4,128]{1,0:T(4,128)S(1)}, f32[128,4,128]{2,0,1:T(8,128)S(1)}) %tuple.105, (s32[2048]{0:T(1024)S(1)}, s32[1,128]{1,0:T(1,128)S(1)}, s32[2048]{0:T(1024)S(1)}, s32[4,128]{1,0:T(4,128)S(1)}, s32[]{:T(128)}, ...), branch_computations={%region_10.10_spmd, %region_11.13_spmd} | conditional | flops 549324288 | bytes 26912820 | solution.py:113
  188.1 3.7 %conditional.3 = (f32[1,4,128]{2,1,0:T(4,128)S(1)}, f32[1,128,4,128]{3,1,2,0:T(8,128)S(1)}) conditional(s32[]{:T(128)} %convert_element_type.82, (f32[4,128]{1,0:T(4,128)S(1)}, f32[128,4,128]{2,0,1:T(8,128)S(1)}) %tuple.105, (s32[2048]{0:T(1024)S(1)}, s32[1,128]{1,0:T(1,128)S(1)}, s32[2048]{0:T(1024)S(1)}, s32[4,128]{1,0:T(4,128)S(1)}, s32[]{:T(128)}, ...), branch_computations={%region_10.10_spmd, %region_11.13_spmd} | conditional | flops 549324288 | bytes 26912820 | solution.py:113
  190.6 1.2 fusion.31
  192.7 1.3 divide_convert_fusion
  194.0 25.9 %while.34 = (s32[]{:T(128)}, bf16[4,128,4096]{2,1,0:T(8,128)(2,1)}, bf16[4,128,512]{1,2,0:T(8,128)(2,1)S(1)}, s32[4]{0:T(128)S(1)}, bf16[3,512,4096]{2,1,0:T(8,128)(2,1)}, /*index=5*/s32[]{:T(128)}, s32[]{:T(128)}, s32[]{:T(128)}) while((s32[]{:T(128)}, bf16[4,128,4096]{2,1,0:T(8,128)(2,1)}, bf16[4,128,512]{1,2,0:T(8,128)(2,1)S(1)}, ...), condition=%wide.region_16.17_spmd, body=%wide.region_15.16_spmd.sunk | while | flops 536870912 | bytes 6423687 | solution.py:127
  196.5 3.9 %fusion.68 = bf16[4,128,4096]{2,1,0:T(8,128)(2,1)} fusion(bf16[4,128,4096]{2,1,0:T(8,128)(2,1)} %get-tuple-element.517, s32[]{:T(128)} %get-tuple-element.516, bf16[3,512,4096]{2,1,0:T(8,128)(2,1)} %get-tuple-element.528, s32[]{:T(128)S(6)} %select_n.82, bf16[4,128,512]{1,2,0:T(8,128)(2,1)S(1)} %get-tuple-element.526), kind=kOutput, calls=%fused_computation.36.clone.1 | convolution fusion | flops 536870912 | bytes 6423556 | tf_op jit(solution)/shard_map/while/body/eval_jaxpr/dot_general | solution.py:125
  203.0 4.0 %fusion.68 = bf16[4,128,4096]{2,1,0:T(8,128)(2,1)} fusion(bf16[4,128,4096]{2,1,0:T(8,128)(2,1)} %get-tuple-element.517, s32[]{:T(128)} %get-tuple-element.516, bf16[3,512,4096]{2,1,0:T(8,128)(2,1)} %get-tuple-element.528, s32[]{:T(128)S(6)} %select_n.82, bf16[4,128,512]{1,2,0:T(8,128)(2,1)S(1)} %get-tuple-element.526), kind=kOutput, calls=%fused_computation.36.clone.1 | convolution fusion | flops 536870912 | bytes 6423556 | tf_op jit(solution)/shard_map/while/body/eval_jaxpr/dot_general | solution.py:125
  209.5 3.9 %fusion.68 = bf16[4,128,4096]{2,1,0:T(8,128)(2,1)} fusion(bf16[4,128,4096]{2,1,0:T(8,128)(2,1)} %get-tuple-element.517, s32[]{:T(128)} %get-tuple-element.516, bf16[3,512,4096]{2,1,0:T(8,128)(2,1)} %get-tuple-element.528, s32[]{:T(128)S(6)} %select_n.82, bf16[4,128,512]{1,2,0:T(8,128)(2,1)S(1)} %get-tuple-element.526), kind=kOutput, calls=%fused_computation.36.clone.1 | convolution fusion | flops 536870912 | bytes 6423556 | tf_op jit(solution)/shard_map/while/body/eval_jaxpr/dot_general | solution.py:125
  216.0 3.9 %fusion.68 = bf16[4,128,4096]{2,1,0:T(8,128)(2,1)} fusion(bf16[4,128,4096]{2,1,0:T(8,128)(2,1)} %get-tuple-element.517, s32[]{:T(128)} %get-tuple-element.516, bf16[3,512,4096]{2,1,0:T(8,128)(2,1)} %get-tuple-element.528, s32[]{:T(128)S(6)} %select_n.82, bf16[4,128,512]{1,2,0:T(8,128)(2,1)S(1)} %get-tuple-element.526), kind=kOutput, calls=%fused_computation.36.clone.1 | convolution fusion | flops 536870912 | bytes 6423556 | tf_op jit(solution)/shard_map/while/body/eval_jaxpr/dot_general | solution.py:125
  219.9 48.1 %reduce-scatter.2.cloned.1.call-done = bf16[64,4096]{1,0:T(8,128)(2,1)} async-done(((bf16[512,4096]{1,0:T(8,128)(2,1)}), bf16[64,4096]{1,0:T(8,128)(2,1)}) %reduce-scatter.2.cloned.1.call-update) | async-done | bytes 524304 | tf_op jit(solution)/shard_map/reduce_scatter | solution.py:130
  268.0 2.0 fusion.51
  (119 shorter events, 32.5 us)
Async XLA Ops:
  6.5 5.5 %copy-start.2 = (s32[16]{0:T(128)S(1)}, s32[16]{0:T(128)}, u32[]{:S(2)}) copy-start(s32[16]{0:T(128)} %param.18) | copy-start | bytes 196
  6.5 55.2 %all-gather.4.cloned.1.call-start = ((), (), s32[]{:S(2)}) async-start(), calls=%async_computation.1 | async-start | bytes 4718592 | tf_op jit(solution)/shard_map/all_gather | solution.py:38
  12.0 152.9 %all-gather.6.cloned.1.call-start = ((), (), s32[]{:S(2)}) async-start(), calls=%async_computation.3 | async-start | bytes 2621440 | tf_op jit(solution)/shard_map/all_gather | solution.py:78
  99.9 46.4 %copy-start.3 = (s32[4]{0:T(128)S(1)}, s32[4]{0:T(128)}, u32[]{:S(2)}) copy-start(s32[4]{0:T(128)} %param.19) | copy-start | bytes 52
  101.5 166.5 %reduce-scatter.2.cloned.1.call-start = ((), (), s32[]{:S(2)}) async-start(), calls=%async_computation.2 | async-start | bytes 4718592 | tf_op jit(solution)/shard_map/reduce_scatter | solution.py:130
  101.6 20.6 %collective-permute-start = (bf16[512,4,128]{0,2,1:T(8,128)(2,1)S(1)}, bf16[512,4,128]{0,2,1:T(8,128)(2,1)S(1)}, u32[]{:S(2)}, u32[]{:S(2)}) collective-permute-start(bf16[512,4,128]{0,2,1:T(8,128)(2,1)S(1)} %get-tuple-element.317), channel_id=1, source_target_pairs={{0,8},{8,16},{16,24},{24,0},{1,9},{9,17},{17,25},{25,1},{2,10},{10... | collective-permute-start | bytes 1572872 | tf_op jit(solution)/shard_map/ppermute | solution.py:74
  122.2 22.8 %collective-permute-start.1 = (bf16[512,4,128]{0,2,1:T(8,128)(2,1)S(1)}, bf16[512,4,128]{0,2,1:T(8,128)(2,1)S(1)}, u32[]{:S(2)}, u32[]{:S(2)}) collective-permute-start(bf16[512,4,128]{0,2,1:T(8,128)(2,1)S(1)} %collective-permute-done), channel_id=1, source_target_pairs={{0,8},{8,16},{16,24},{24,0},{1,9},{9,17},{17,25},{25,1},{2,10},{10... | collective-permute-start | bytes 1572872 | tf_op jit(solution)/shard_map/ppermute | solution.py:74
  145.0 12.5 %collective-permute-start.2 = (bf16[512,4,128]{0,2,1:T(8,128)(2,1)S(1)}, bf16[512,4,128]{0,2,1:T(8,128)(2,1)}, u32[]{:S(2)}, u32[]{:S(2)}) collective-permute-start(bf16[512,4,128]{0,2,1:T(8,128)(2,1)S(1)} %collective-permute-done.1), channel_id=1, source_target_pairs={{0,8},{8,16},{16,24},{24,0},{1,9},{9,17},{17,25},{25,1},{2,10},{10... | collective-permute-start | bytes 1572872 | tf_op jit(solution)/shard_map/ppermute | solution.py:74
  170.6 2.2 copy-start.1
  176.5 2.2 copy-start.1
  182.4 2.2 copy-start.1
  188.4 2.2 copy-start.1
  219.9 48.1 %copy-start = (bf16[64,4096]{1,0:T(8,128)(2,1)S(1)}, bf16[64,4096]{1,0:T(8,128)(2,1)}, u32[]{:S(2)}) copy-start(bf16[64,4096]{1,0:T(8,128)(2,1)} %param.14) | copy-start | bytes 1572868
Sparse Core Ops, SparseCore 0:
  12.1 49.5 all-gather.3
  101.7 47.1 all-gather.5
  220.1 47.9 reduce-scatter.1
